TPU v7x, 32 devices: a whole 2x2x4 slice. The times are simulated.
32 devices in a mesh: grp: 8 (over y, x, core), blk: 4 (over z).
Axes of the slice: x: 2, y: 2, z: 4, core: 2. Of those that a mesh axis runs over, the one named last changes fastest.
Arguments:
- tokens: bfloat16 [256, 6144], P(('grp', 'blk')), may hold values from -6 to 6
- norm_gain: bfloat16 [6144], replicated, may hold values from 0.099609375 to 1.8984375
- expert_ids: int32 [256, 2], P(('grp', 'blk')), may hold values from 0 to 7, all different within a row; in each aligned block of 8 rows (0 to 7, 8 to 15, ...) at most 3 rows name the same one
- combine: float32 [256, 2], P(('grp', 'blk')), may hold values from 0.2 to 1
- w_gate: bfloat16 [6144, 65536], P(None, ('grp', 'blk')), may hold values from -0.078125 to 0.078125
- w_up: bfloat16 [6144, 65536], P(None, ('grp', 'blk')), may hold values from -0.078125 to 0.078125
- w_down: bfloat16 [65536, 6144], P(('grp', 'blk')), may hold values from -0.0625 to 0.0625
Outputs:
- layer_out: bfloat16 [256, 6144], P(('grp', 'blk'))
Inputs may be any that keep to these rules, and one draw needn't show every extreme that they name: `expert_ids`: each row names 2 different experts; in the rows of one device no expert is named more than 3 times, a bound that some block reaches.
All inputs are finite; a program needn't handle non-finite values.
Results may differ from a plain program's by a relative error of at most 0.0075.
Values may be sent and summed in bfloat16 or wider, within the bound.
A program may use at most 128 MiB of HBM per device.

v0:
```python
import jax
import jax.numpy as jnp
from jax import lax
from jax.sharding import PartitionSpec as P

E = 8
TOP = 2
CAP = 3


epsilon = 1e-05


def on_device(tokens, norm_gain, expert_ids, combine, w_gate, w_up, w_down):
    group_count = lax.axis_size("grp")
    per_group = group_count // E
    tok_count = tokens.shape[0]
    model_width = tokens.shape[1]
    wide_tokens = tokens.astype(jnp.float32)
    scale_rows = lax.rsqrt(jnp.mean(wide_tokens * wide_tokens, axis=1, keepdims=True) + epsilon)
    normed = (wide_tokens * scale_rows * norm_gain.astype(jnp.float32)[None, :]).astype(
        jnp.bfloat16
    )
    pair_rows = jnp.repeat(normed, TOP, axis=0)
    route_ids = expert_ids.reshape(tok_count * TOP)
    one_hot = (route_ids[:, None] == jnp.arange(E, dtype=jnp.int32)[None, :]).astype(jnp.int32)
    earlier = jnp.cumsum(one_hot, axis=0) - one_hot
    slot_index = jnp.sum(earlier * one_hot, axis=1)
    slot_match = (
        slot_index[None, None, :] == jnp.arange(CAP, dtype=jnp.int32)[None, :, None]
    ).astype(jnp.int32)
    placer = (one_hot.T[:, None, :] * slot_match).astype(jnp.bfloat16)
    buffer = jnp.einsum(
        "ecp,pd->ecd", placer, pair_rows, preferred_element_type=jnp.float32
    ).astype(jnp.bfloat16)
    outgoing = jnp.repeat(buffer, per_group, axis=0)
    arrived = lax.all_to_all(outgoing, "grp", split_axis=0, concat_axis=0, tiled=True)
    flat_rows = arrived.reshape(group_count * CAP, model_width)
    shard_rows = lax.all_gather(flat_rows, "blk", axis=0, tiled=True)
    gate_val = jnp.dot(shard_rows, w_gate, preferred_element_type=jnp.float32)
    up_val = jnp.dot(shard_rows, w_up, preferred_element_type=jnp.float32)
    hidden = (jax.nn.silu(gate_val) * up_val).astype(jnp.bfloat16)
    partial_value = jnp.dot(hidden, w_down, preferred_element_type=jnp.float32)
    rounded = lax.optimization_barrier(partial_value.astype(jnp.bfloat16))
    own_rows = lax.psum_scatter(
        rounded.astype(jnp.float32).astype(jnp.bfloat16), "blk", scatter_dimension=0, tiled=True
    ).astype(jnp.float32)
    home_terms = own_rows.reshape(group_count, CAP, model_width)
    returned = lax.all_to_all(
        home_terms.astype(jnp.bfloat16), "grp", split_axis=0, concat_axis=0, tiled=True
    ).astype(home_terms.dtype)
    expert_out = jnp.sum(returned.reshape(E, per_group, CAP, model_width), axis=1)
    pair_out = expert_out.reshape(E * CAP, model_width)[route_ids * CAP + slot_index]
    expert_mix = jnp.sum(
        pair_out.reshape(tok_count, TOP, model_width) * combine[:, :, None], axis=1
    )
    return (wide_tokens + expert_mix).astype(jnp.bfloat16)


def solution(mesh):
    return jax.shard_map(
        on_device,
        mesh=mesh,
        in_specs=(
            P(("grp", "blk"), None),
            P(),
            P(("grp", "blk"), None),
            P(("grp", "blk"), None),
            P(None, ("grp", "blk")),
            P(None, ("grp", "blk")),
            P(("grp", "blk"), None),
        ),
        out_specs=P(("grp", "blk"), None),
        check_vma=False,
    )
```

profile of v0, /device:TPU:0, one launch (start us, length us, event | category | flops | bytes accessed | tf_op | source)
XLA Modules:
  0.0 140.3 jit_solution(3848089059625305075)
XLA Ops:
  6.5 0.0 all-gather.2.cloned.1.call-start
  6.5 0.8 copy.15
  7.3 0.1 eq.44
  7.4 0.1 fusion.11
  7.5 0.2 select_reduce_fusion
  7.7 0.7 convert_element_type.55
  8.4 1.1 fusion.7
  9.5 1.0 fusion.9
  10.5 0.1 broadcast_in_dim.2
  10.6 0.1 reshape.123
  10.6 0.2 convolution_convert_fusion.1
  10.9 0.3 copy.16
  11.1 13.3 %all_to_all.10 = bf16[8,3,6144]{2,1,0:T(4,128)(2,1)S(1)} all-to-all(bf16[8,3,6144]{2,1,0:T(4,128)(2,1)S(1)} %copy.16), channel_id=1, replica_groups=mesh['grp'=8,'blk'=4] {'grp'}, dimensions={0} | all-to-all | bytes 589824 | tf_op jit(solution)/shard_map/all_to_all | solution.py:37
  24.4 1.0 reshape.109
  25.4 0.0 all-gather.2.cloned.1.call-update
  25.4 0.0 reduce-scatter.2.cloned.1.call-start
  25.5 29.7 %all-gather.2.cloned.1.call-done = bf16[96,6144]{1,0:T(8,128)(2,1)} async-done(((bf16[24,6144]{1,0:T(8,128)(2,1)}), bf16[96,6144]{1,0:T(8,128)(2,1)}) %all-gather.2.cloned.1.call-update) | async-done | bytes 1179664 | tf_op jit(solution)/shard_map/all_gather | solution.py:39
  55.2 0.0 copy-start
  55.2 12.6 %fusion.18 = f32[96,2048]{1,0:T(8,128)S(1)} fusion(bf16[96,6144]{1,0:T(8,128)(2,1)} %all-gather.2.cloned.1.call-done, bf16[6144,2048]{1,0:T(8,128)(2,1)} %param.11), kind=kOutput, calls=%fused_computation.36 | convolution fusion | flops 2415919104 | bytes 27131904 | tf_op jit(solution)/shard_map/dot_general | solution.py:40
  67.8 0.0 copy-done
  67.8 0.0 copy-start.2
  67.8 0.0 copy-start.3
  67.9 0.0 copy-start.1
  67.9 20.7 %convolution_convert_fusion = bf16[96,6144]{1,0:T(8,128)(2,1)} fusion(bf16[2048,6144]{1,0:T(8,128)(2,1)} %param.13, bf16[96,6144]{1,0:T(8,128)(2,1)S(1)} %copy-done, bf16[6144,2048]{1,0:T(8,128)(2,1)} %param.12, f32[96,2048]{1,0:T(8,128)S(1)} %fusion.18), kind=kOutput, calls=%fused_computation.1 | convolution fusion | flops 4833607680 | bytes 53477376 | tf_op jit(solution)/shard_map/dot_general | solution.py:43
  88.5 0.0 reduce-scatter.2.cloned.1.call-update
  88.5 0.0 copy-done.2
  88.6 0.1 copy.17
  88.6 0.1 mul.75
  88.7 0.0 copy-done.3
  88.7 0.1 copy.18
  88.8 28.4 %reduce-scatter.2.cloned.1.call-done = bf16[24,6144]{1,0:T(8,128)(2,1)} async-done(((bf16[96,6144]{1,0:T(8,128)(2,1)}), bf16[24,6144]{1,0:T(8,128)(2,1)}) %reduce-scatter.2.cloned.1.call-update) | async-done | bytes 294928 | tf_op jit(solution)/shard_map/reduce_scatter | solution.py:45
  117.2 1.9 %convert_element_type.60 = bf16[8,3,6144]{2,1,0:T(4,128)(2,1)} reshape(bf16[24,6144]{1,0:T(8,128)(2,1)} %reduce-scatter.2.cloned.1.call-done) | data formatting | bytes 589824 | tf_op jit(solution)/shard_map/convert_element_type | solution.py:50
  119.1 3.7 %all-to-all-start.1 = ((bf16[8,3,6144]{2,1,0:T(4,128)(2,1)}), bf16[8,3,6144]{2,1,0:T(4,128)(2,1)S(1)}, u32[]{:S(2)}, u32[]{:S(2)}) async-start(bf16[8,3,6144]{2,1,0:T(4,128)(2,1)} %convert_element_type.60), calls=%async_computation.2 | async-start | bytes 786432 | tf_op jit(solution)/shard_map/all_to_all | solution.py:49
  122.8 8.3 %all-to-all-done.1 = bf16[8,3,6144]{2,1,0:T(4,128)(2,1)S(1)} async-done(((bf16[8,3,6144]{2,1,0:T(4,128)(2,1)}), bf16[8,3,6144]{2,1,0:T(4,128)(2,1)S(1)}, u32[]{:S(2)}, u32[]{:S(2)}) %all-to-all-start.1) | async-done | bytes 294944 | tf_op jit(solution)/shard_map/all_to_all | solution.py:49
  131.1 0.2 reshape.114
  131.3 0.7 gather_fusion
  132.0 0.2 reshape.112
  132.2 0.6 multiply_reduce_fusion
  132.8 0.0 copy-done.1
  132.8 0.7 fusion.10
  (7 shorter events, 0.1 us)
Async XLA Ops:
  6.5 48.7 %all-gather.2.cloned.1.call-start = ((), (), s32[]{:S(2)}) async-start(), calls=%async_computation.3 | async-start | bytes 1474560 | tf_op jit(solution)/shard_map/all_gather | solution.py:39
  25.4 91.8 %reduce-scatter.2.cloned.1.call-start = ((), (), s32[]{:S(2)}) async-start(), calls=%async_computation.4 | async-start | bytes 1474560 | tf_op jit(solution)/shard_map/reduce_scatter | solution.py:45
  55.2 12.6 %copy-start = (bf16[96,6144]{1,0:T(8,128)(2,1)S(1)}, bf16[96,6144]{1,0:T(8,128)(2,1)}, u32[]{:S(2)}) copy-start(bf16[96,6144]{1,0:T(8,128)(2,1)} %all-gather.2.cloned.1.call-done) | copy-start | bytes 3538948
  67.8 20.7 %copy-start.2 = (s32[8,2]{0,1:T(2,128)S(1)}, s32[8,2]{0,1:T(2,128)}, u32[]{:S(2)}) copy-start(s32[8,2]{0,1:T(2,128)} %param.9) | copy-start | bytes 196
  67.8 20.9 %copy-start.3 = (f32[8,2]{0,1:T(2,128)S(1)}, f32[8,2]{0,1:T(2,128)}, u32[]{:S(2)}) copy-start(f32[8,2]{0,1:T(2,128)} %param.10) | copy-start | bytes 196
  67.9 64.9 %copy-start.1 = (bf16[8,6144]{1,0:T(8,128)(2,1)S(1)}, bf16[8,6144]{1,0:T(8,128)(2,1)}, u32[]{:S(2)}) copy-start(bf16[8,6144]{1,0:T(8,128)(2,1)} %param.7) | copy-start | bytes 294916
  119.1 12.0 %all-to-all-start.1 = ((bf16[8,3,6144]{2,1,0:T(4,128)(2,1)}), bf16[8,3,6144]{2,1,0:T(4,128)(2,1)S(1)}, u32[]{:S(2)}, u32[]{:S(2)}) async-start(bf16[8,3,6144]{2,1,0:T(4,128)(2,1)} %convert_element_type.60), calls=%async_computation.2 | async-start | bytes 786432 | tf_op jit(solution)/shard_map/all_to_all | solution.py:49
Sparse Core Ops, SparseCore 0:
  25.6 29.6 all-gather.1
  88.7 28.5 reduce-scatter.1
where the time goes:
time: 141 us; the launch traced here: 140 us
  waiting for transfers between devices  66.5 us (47%)
  matrix products  33.5 us (24%)
  between operations  13.5 us (10%)
  blocking collectives  13.3 us (9%)
  local copies, waits for them, and re-layouts  5.51 us (4%)
  other arithmetic  4.3 us (3%)
  starting transfers between devices  3.7 us (3%)
    all_gather x1, waiting for transfers between devices, on_device(): shard_rows = lax.all_gather(flat_rows, 'blk', axis=0, tiled=True)  29.7 us
    reduce_scatter x1, waiting for transfers between devices, on_device(): lax.psum_scatter(rounded.astype(jnp.float32).astype(jnp.bfloat16), 'blk',...  28.4 us
    dot_general x1, matrix products, on_device(): partial_value = jnp.dot(hidden, w_down, preferred_element_type=jnp.float32)  20.7 us
    all_to_all x1, blocking collectives, on_device(): lax.all_to_all(outgoing, 'grp', split_axis=0, concat_axis=0, tiled=True)  13.3 us
    dot_general x1, matrix products, on_device(): gate_val = jnp.dot(shard_rows, w_gate, preferred_element_type=jnp.float32)  12.6 us
    all_to_all x1, waiting for transfers between devices, on_device(): lax.all_to_all(home_terms.astype(jnp.bfloat16), 'grp', split_axis=0, conc...  8.29 us
    all_to_all x1, starting transfers between devices, on_device(): lax.all_to_all(home_terms.astype(jnp.bfloat16), 'grp', split_axis=0, conc...  3.65 us
  transfers between devices with their start and end apart: 3, of which 3 were waited for; matrix products, arithmetic and copies ran while one was open for 0% of the time, Pallas kernels for 0%

commit v1 on v0

--- a/solution.py
+++ b/solution.py
@@ -1,6 +1,10 @@
+import functools
+import numpy as np
 import jax
 import jax.numpy as jnp
 from jax import lax
+from jax.experimental import pallas as pl
+from jax.experimental.pallas import tpu as pltpu
 from jax.sharding import PartitionSpec as P
 
 E = 8
@@ -9,12 +13,273 @@
 
 
 epsilon = 1e-05
+VMEM_LIMIT = 67_000_000
+BF16, F32 = jnp.bfloat16, jnp.float32
+
+
+def xor_index(index, offset, count):
+    total, bit = 0, 1
+    while bit < count:
+        digit = (index // bit) % 2
+        total = total + bit * ((1 - digit) if offset & bit else digit)
+        bit *= 2
+    return total
+
+
+def tables(groups, blocks, splits, pair):
+    lane = np.arange(groups * splits * CAP)
+    send = [lane // (splits * CAP), (lane // CAP) % splits, lane % CAP]
+    lane = np.arange(groups * pair * blocks * CAP)
+    back = [lane // (pair * blocks * CAP), (lane // (blocks * CAP)) % pair, (lane // CAP) % blocks, lane % CAP]
+    sources = 2 * groups
+    gather = np.zeros((sources * splits * CAP,) * 2, np.float32)
+    for q in range(splits):
+        for s in range(sources):
+            for c in range(CAP):
+                gather[(q * sources + s) * CAP + c, (s * splits + q) * CAP + c] = 1
+    rows = pair * blocks * groups * CAP
+    spread = np.zeros((rows, rows), np.float32)
+    for k in range(groups):
+        for v in range(pair):
+            for d in range(blocks):
+                for c in range(CAP):
+                    spread[((k * pair + v) * blocks + d) * CAP + c, ((v * blocks + d) * groups + k) * CAP + c] = 1
+    return np.array(send, np.int32), np.array(back, np.int32), gather, spread
+
+
+def layer_kernel(cfg, tok_ref, gain_ref, ids_ref, comb_ref, send_tab, back_tab, gather_ref, spread_ref,
+                 wg_ref, wu_ref, wd_ref, out_ref,
+                 gbuf, ubuf, dbuf, meta, toks, sbuf, rbuf, xbuf, gacc, uacc, hid, obuf, pbuf, qbuf, ybuf, vbuf,
+                 wsem, msem, mrsem, tsem, trsem, ssem, srsem, psem, prsem, ysem, yrsem):
+    groups, blocks, splits, pair, gslots, dslots = cfg
+    me, depth = lax.axis_index("grp"), lax.axis_index("blk")
+    tok_count, width = tok_ref.shape
+    part = width // splits
+    units = wg_ref.shape[1]
+    unit_rows = splits * CAP
+    back_rows = pair * blocks * CAP
+    rows = blocks * groups * CAP
+
+    def weights(kind, q):
+        if kind == 0:
+            return pltpu.make_async_copy(wg_ref.at[pl.ds(q * part, part)], gbuf.at[q % gslots], wsem.at[0, q])
+        if kind == 1:
+            return pltpu.make_async_copy(wu_ref.at[pl.ds(q * part, part)], ubuf.at[q % gslots], wsem.at[1, q])
+        return pltpu.make_async_copy(wd_ref.at[:, pl.ds(q * part, part)], dbuf.at[q % dslots], wsem.at[2, q])
+
+    for q in range(gslots):
+        weights(0, q).start()
+        weights(1, q).start()
+    for q in range(dslots):
+        weights(2, q).start()
+
+    group_of = [{"grp": xor_index(me, k, groups), "blk": depth} for k in range(groups)]
+    block_of = [{"grp": me, "blk": xor_index(depth, d, blocks)} for d in range(blocks)]
+    barrier = pltpu.get_barrier_semaphore()
+    for peer in group_of[1:] + block_of[1:]:
+        pl.semaphore_signal(barrier, inc=1, device_id=peer, device_id_type=pl.DeviceIdType.MESH)
+
+    lane = lax.broadcasted_iota(jnp.int32, (tok_count, 128), 1)
+    ids = ids_ref[...].astype(F32)
+    comb = comb_ref[...]
+    meta[0] = jnp.where(lane == 0, ids[:, 0:1], jnp.where(lane == 1, ids[:, 1:2],
+                        jnp.where(lane == 2, comb[:, 0:1], jnp.where(lane == 3, comb[:, 1:2], 0.0))))
+    wide = tok_ref[...].astype(F32)
+    scale = lax.rsqrt(jnp.mean(wide * wide, axis=1, keepdims=True) + epsilon)
+    normed = wide * scale * gain_ref[...].astype(F32)
+    toks[0] = jnp.concatenate([normed[:, q * part:(q + 1) * part] for q in range(splits)], axis=0).astype(BF16)
+    pl.semaphore_wait(barrier, groups + blocks - 2)
+
+    def remote(src, dst, send, recv, peer):
+        return pltpu.make_async_remote_copy(src_ref=src, dst_ref=dst, send_sem=send, recv_sem=recv,
+                                            device_id=peer, device_id_type=pl.DeviceIdType.MESH)
+
+    meta_out = [None] + [remote(meta.at[0], meta.at[d], msem.at[d], mrsem.at[d], block_of[d]) for d in range(1, blocks)]
+    toks_out = [None] + [remote(toks.at[0], toks.at[d], tsem.at[d], trsem.at[d], block_of[d]) for d in range(1, blocks)]
+    for d in range(1, blocks):
+        meta_out[d].start()
+        toks_out[d].start()
+
+    def matches(info, expert, slot):
+        first = expert == info[:, 0:1]
+        second = expert == info[:, 1:2]
+        member = jnp.where(first, 1.0, jnp.where(second, 1.0, 0.0))
+        row = lax.broadcasted_iota(jnp.int32, member.shape, 0)
+        earlier = jnp.zeros_like(member)
+        for t in range(tok_count - 1):
+            earlier = earlier + jnp.where(row > t, member[t:t + 1, :], 0.0)
+        at_slot = jnp.where(earlier == slot, 1.0, 0.0)
+        return jnp.where(first, at_slot, 0.0), jnp.where(second, at_slot, 0.0)
+
+    send_expert = (send_tab[0:1, :] ^ me).astype(F32)
+    send_split, send_slot = send_tab[1:2, :], send_tab[2:3, :].astype(F32)
+    back_expert = (back_tab[0:1, :] ^ me).astype(F32)
+    back_pair, back_depth, back_slot = back_tab[1:2, :], back_tab[2:3, :], back_tab[3:4, :].astype(F32)
+
+    slots_out = {}
+    for d in range(blocks):
+        if d:
+            meta_out[d].wait_recv()
+            toks_out[d].wait_recv()
+        one, two = matches(meta[d], send_expert, send_slot)
+        both = one + two
+        placer = jnp.concatenate([jnp.where(send_split == q, both, 0.0) for q in range(splits)], axis=0).astype(BF16)
+        placed = lax.dot_general(placer, toks[d], (((0,), (0,)), ((), ())), preferred_element_type=F32)
+        for k in range(1, groups):
+            sbuf[d, k] = placed[k * unit_rows:(k + 1) * unit_rows].astype(BF16)
+        rbuf[d, 0] = placed[:unit_rows].astype(BF16)
+        for k in range(groups - 1, 0, -1):
+            slots_out[d, k] = remote(sbuf.at[d, k], rbuf.at[d, k], ssem.at[d, k], srsem.at[d, k], group_of[k])
+            slots_out[d, k].start()
+
+    mixes = []
+    for d in range(blocks):
+        one, two = matches(meta[d], back_expert, back_slot)
+        mix = jnp.where(back_depth == d, one * meta[d][:, 2:3] + two * meta[d][:, 3:4], 0.0)
+        mixes += [jnp.where(back_pair == v, mix, 0.0) for v in range(pair)]
+    mix = jnp.concatenate(mixes, axis=0)
+    mix_high = mix.astype(BF16)
+    mix_low = (mix - mix_high.astype(F32)).astype(BF16)
+
+    half = 2 * groups * CAP
+    for h in range(blocks // 2):
+        for d in (2 * h, 2 * h + 1):
+            for k in range(1, groups):
+                slots_out[d, k].wait_recv()
+        held = jnp.concatenate([rbuf[d, k].astype(F32) for d in (2 * h, 2 * h + 1) for k in range(groups)], axis=0).astype(BF16)
+        sorted_rows = jnp.dot(gather_ref[...], held, preferred_element_type=F32).astype(BF16)
+        for q in range(splits):
+            xbuf[q, h * half:(h + 1) * half, :] = sorted_rows[q * half:(q + 1) * half]
+
+    tile = min(units, 512)
+    gacc[...] = jnp.zeros_like(gacc)
+    uacc[...] = jnp.zeros_like(uacc)
+    for q in range(splits):
+        weights(0, q).wait()
+        weights(1, q).wait()
+
+        @pl.loop(0, units // tile)
+        def _(n):
+            cols = pl.ds(pl.multiple_of(n * tile, tile), tile)
+            gacc[:, cols] += jnp.dot(xbuf[q], gbuf[q % gslots, :, cols], preferred_element_type=F32)
+            uacc[:, cols] += jnp.dot(xbuf[q], ubuf[q % gslots, :, cols], preferred_element_type=F32)
+
+        if q + gslots < splits:
+            weights(0, q + gslots).start()
+            weights(1, q + gslots).start()
+
+    @pl.loop(0, units // tile)
+    def _(n):
+        cols = pl.ds(pl.multiple_of(n * tile, tile), tile)
+        gate = gacc[:, cols]
+        hid[:, cols] = (gate / (1.0 + jnp.exp(-gate)) * uacc[:, cols]).astype(BF16)
+
+    back_out = {}
+    steps = splits // pair
+    for j in range(steps):
+        for v in range(pair):
+            q = j * pair + v
+            weights(2, q).wait()
+
+            @pl.loop(0, part // 256)
+            def _(n):
+                cols = pl.ds(pl.multiple_of(n * 256, 256), 256)
+                obuf[v * rows:(v + 1) * rows, cols] = jnp.dot(
+                    hid[...], dbuf[q % dslots, :, cols], preferred_element_type=F32).astype(BF16)
+
+            if q + dslots < splits:
+                weights(2, q + dslots).start()
+        spread = jnp.dot(spread_ref[...], obuf[...], preferred_element_type=F32)
+        for k in range(1, groups):
+            pbuf[j, k] = spread[k * back_rows:(k + 1) * back_rows].astype(BF16)
+        qbuf[j, 0] = spread[:back_rows].astype(BF16)
+        for k in range(groups - 1, 0, -1):
+            back_out[j, k] = remote(pbuf.at[j, k], qbuf.at[j, k], psem.at[j, k], prsem.at[j, k], group_of[k])
+            back_out[j, k].start()
+
+    mixed_out, own = {}, []
+    span = pair * tok_count
+    for j in range(steps):
+        for k in range(1, groups):
+            back_out[j, k].wait_recv()
+        held = jnp.concatenate([qbuf[j, k].astype(F32) for k in range(groups)], axis=0).astype(BF16)
+        mixed = (jnp.dot(mix_high, held, preferred_element_type=F32)
+                 + jnp.dot(mix_low, held, preferred_element_type=F32))
+        own.append(mixed[:span])
+        for d in range(1, blocks):
+            ybuf[j, d] = mixed[d * span:(d + 1) * span].astype(BF16)
+        for d in range(1, blocks):
+            mixed_out[j, d] = remote(ybuf.at[j, d], vbuf.at[j, d], ysem.at[j, d], yrsem.at[j, d], block_of[d])
+            mixed_out[j, d].start()
+
+    for j in range(steps):
+        total = own[j]
+        for d in range(1, blocks):
+            mixed_out[j, d].wait_recv()
+            total = total + vbuf[j, d].astype(F32)
+        for v in range(pair):
+            cols = slice((j * pair + v) * part, (j * pair + v + 1) * part)
+            out_ref[:, cols] = (tok_ref[:, cols].astype(F32) + total[v * tok_count:(v + 1) * tok_count]).astype(BF16)
+
+    for copies in (meta_out[1:], toks_out[1:], slots_out.values(), back_out.values(), mixed_out.values()):
+        for copy in copies:
+            copy.wait_send()
+
+
+def fused(groups, blocks, tokens, norm_gain, expert_ids, combine, w_gate, w_up, w_down):
+    tok_count, width = tokens.shape
+    units = w_gate.shape[1]
+    splits, pair = 8, 2
+    gslots, dslots = 6, 4
+    part = width // splits
+    rows = blocks * groups * CAP
+    steps = splits // pair
+    send, back, gather, spread = tables(groups, blocks, splits, pair)
+    vmem = pl.BlockSpec(memory_space=pltpu.VMEM)
+    dma = pltpu.SemaphoreType.DMA
+    unit_rows, back_rows, span = splits * CAP, pair * blocks * CAP, pair * tok_count
+    return pl.pallas_call(
+        functools.partial(layer_kernel, (groups, blocks, splits, pair, gslots, dslots)),
+        out_shape=jax.ShapeDtypeStruct((tok_count, width), BF16),
+        in_specs=[vmem] * 8 + [pl.BlockSpec(memory_space=pl.ANY)] * 3,
+        out_specs=vmem,
+        scratch_shapes=[
+            pltpu.VMEM((gslots, part, units), BF16),
+            pltpu.VMEM((gslots, part, units), BF16),
+            pltpu.VMEM((dslots, units, part), BF16),
+            pltpu.VMEM((blocks, tok_count, 128), F32),
+            pltpu.VMEM((blocks, splits * tok_count, part), BF16),
+            pltpu.VMEM((blocks, groups, unit_rows, part), BF16),
+            pltpu.VMEM((blocks, groups, unit_rows, part), BF16),
+            pltpu.VMEM((splits, rows, part), BF16),
+            pltpu.VMEM((rows, units), F32),
+            pltpu.VMEM((rows, units), F32),
+            pltpu.VMEM((rows, units), BF16),
+            pltpu.VMEM((pair * rows, part), BF16),
+            pltpu.VMEM((steps, groups, back_rows, part), BF16),
+            pltpu.VMEM((steps, groups, back_rows, part), BF16),
+            pltpu.VMEM((steps, blocks, span, part), BF16),
+            pltpu.VMEM((steps, blocks, span, part), BF16),
+            dma((3, splits)),
+            dma((blocks,)), dma((blocks,)), dma((blocks,)), dma((blocks,)),
+            dma((blocks, groups)), dma((blocks, groups)),
+            dma((steps, groups)), dma((steps, groups)),
+            dma((steps, blocks)), dma((steps, blocks)),
+        ],
+        compiler_params=pltpu.CompilerParams(collective_id=0, has_side_effects=True, vmem_limit_bytes=VMEM_LIMIT),
+    )(tokens, norm_gain.reshape(1, width), expert_ids, combine, jnp.asarray(send), jnp.asarray(back),
+      jnp.asarray(gather, BF16), jnp.asarray(spread, BF16), w_gate, w_up, w_down)
 
 
 def on_device(tokens, norm_gain, expert_ids, combine, w_gate, w_up, w_down):
     group_count = lax.axis_size("grp")
+    block_count = lax.axis_size("blk")
     per_group = group_count // E
     tok_count = tokens.shape[0]
+    if group_count == E and block_count == 4 and tok_count == 8 and tokens.shape[1] % 2048 == 0:
+        return fused(
+            group_count, block_count, tokens, norm_gain, expert_ids, combine, w_gate, w_up, w_down
+        )
     model_width = tokens.shape[1]
     wide_tokens = tokens.astype(jnp.float32)
     scale_rows = lax.rsqrt(jnp.mean(wide_tokens * wide_tokens, axis=1, keepdims=True) + epsilon)

time: 141 us -> 67.2 us (0.48)
  waiting for transfers between devices: 66.5 us -> 0 us
  Pallas kernels: 0 us -> 61.3 us
  matrix products: 33.5 us -> 0 us
  between operations: 13.5 us -> 0.01 us
  blocking collectives: 13.3 us -> 0 us
  other arithmetic: 4.3 us -> 0 us
  starting transfers between devices: 3.7 us -> 0 us
    pallas_call x0 -> x1, Pallas kernels: none -> 61.3 us  [fused(): pl.pallas_call(functools.partial(layer_kernel, (groups, blocks, splits, p...]
    dot_general x3 -> x0, matrix products: 33.5 us -> none  [the longest x1 20.7 us: on_device(): partial_value = jnp.dot(hidden, w_down, preferred_element_type=jnp.float32)]
    all_gather x1 -> x0, waiting for transfers between devices: 29.7 us -> none  [on_device(): shard_rows = lax.all_gather(flat_rows, 'blk', axis=0, tiled=True)]
    reduce_scatter x1 -> x0, waiting for transfers between devices: 28.4 us -> none  [on_device(): lax.psum_scatter(rounded.astype(jnp.float32).astype(jnp.bfloat16), 'blk',...]
    all_to_all x1 -> x0, blocking collectives: 13.3 us -> none  [on_device(): lax.all_to_all(outgoing, 'grp', split_axis=0, concat_axis=0, tiled=True)]
    all_to_all x1 -> x0, waiting for transfers between devices: 8.29 us -> none  [on_device(): lax.all_to_all(home_terms.astype(jnp.bfloat16), 'grp', split_axis=0, conc...]
    all_to_all x1 -> x0, starting transfers between devices: 3.65 us -> none  [on_device(): lax.all_to_all(home_terms.astype(jnp.bfloat16), 'grp', split_axis=0, conc...]
    unnamed x10 -> x3, local copies, waits for them, and re-layouts: 0.86 us -> 4.23 us
  transfers between devices with their start and end apart: 3 -> 0, of which waited for: 3 -> 0; matrix products, arithmetic and copies ran while one was open for 0% -> 0% of each run, Pallas kernels for 0% -> 0%
where the time goes in v1:
time: 67.2 us; the launch traced here: 66.9 us
  Pallas kernels  61.3 us (91%)
  local copies, waits for them, and re-layouts  5.56 us (8%)
    pallas_call x1, Pallas kernels, fused(): pl.pallas_call(functools.partial(layer_kernel, (groups, blocks, splits, p...  61.3 us
    unnamed x3, local copies, waits for them, and re-layouts  4.23 us

profile of v1, /device:TPU:0, one launch (start us, length us, event | category | flops | bytes accessed | tf_op | source)
XLA Modules:
  0.0 66.9 jit_solution(6671488886138543288)
XLA Ops:
  0.0 1.3 %copy.12.ids_ref = s32[8,2]{1,0:T(8,128)} copy(s32[8,2]{0,1:T(2,128)} %param.13) | data formatting | bytes 128 | tf_op args[2]
  1.3 1.3 %copy.13.comb_ref = f32[8,2]{1,0:T(8,128)} copy(f32[8,2]{0,1:T(2,128)} %param.14) | data formatting | bytes 128 | tf_op args[3]
  2.7 1.3 %reshape.3.gain_ref = bf16[1,6144]{1,0:T(2,128)(2,1)} reshape(bf16[6144]{0:T(1024)(128)(2,1)} %param.12) | data formatting | bytes 24576 | tf_op jit(solution)/shard_map/reshape | solution.py:270
  4.0 61.3 %shard_map.109 = bf16[8,6144]{1,0:T(8,128)(2,1)} custom-call(bf16[8,6144]{1,0:T(8,128)(2,1)} %tok_ref.1, bf16[1,6144]{1,0:T(2,128)(2,1)} %reshape.3.gain_ref, s32[8,2]{1,0:T(8,128)} %copy.12.ids_ref, f32[8,2]{1,0:T(8,128)} %copy.13.comb_ref, s32[3,192]{1,0:T(4,128)} %constant.8.clone.send_tab, s32[4,192]{1,0:T(4,128)} %constant.9.clone.back_tab, ...), custom_call_target="tpu_custom_call" | custom-call | tf_op jit(solution)/shard_map/pallas_call | solution.py:241
  65.4 1.5 %copy.15 = bf16[8,6144]{1,0:T(8,128)(2,1)} copy(bf16[8,6144]{1,0:T(8,128)(2,1)} %shard_map.109) | data formatting | bytes 196608
